TPU v7x, 32 devices: a whole 2x2x4 slice. The times are simulated.
32 devices in a mesh: seq: 16 (over z, y, x), ch: 2 (over core).
Axes of the slice: x: 2, y: 2, z: 4, core: 2. Of those that a mesh axis runs over, the one named last changes fastest.
Arguments:
- tokens: bfloat16 [2048, 8192], P('seq', 'ch'), may hold values from -6 to 6
- query_in: bfloat16 [2048, 8192], P('seq', 'ch'), may hold values from -6 to 6
- key_in: bfloat16 [2048, 8192], P('seq', 'ch'), may hold values from -6 to 6
- proj_in: bfloat16 [8192, 1536], P('ch', 'seq'), may hold values from -0.0625 to 0.0625
- proj_out: bfloat16 [1536, 8192], P('seq', 'ch'), may hold values from -0.15625 to 0.15625
- short_taps: float32 [3, 7, 8192], P(None, None, 'ch'), may hold values from -2.4 to 2.4
- residues: float32 [16, 8192], P(None, 'ch'), may hold values from -1.8 to 1.8
- mode_rates: float32 [16, 8192], P(None, 'ch'), may hold values from 0.00024414062 to 0.03
- skip_gain: float32 [8192], P('ch'), may hold values from -3 to 3
Outputs:
- operator_out: bfloat16 [2048, 8192], P('seq', 'ch')
All inputs are finite; a program needn't handle non-finite values.
Results may differ from a plain program's by a relative error of at most 0.0069.
Values may be sent and summed in bfloat16 or wider, within the bound.
A program may use at most 192 MiB of HBM per device.

v0:
```python
import functools

import jax
import jax.numpy as jnp
from jax import lax
from jax.experimental import pallas as pl
from jax.experimental.pallas import tpu as pltpu
from jax.sharding import PartitionSpec as P

MESH = pl.DeviceIdType.MESH
VMEM = pl.BlockSpec(memory_space=pltpu.VMEM)
ANY = pl.BlockSpec(memory_space=pl.ANY)
GROUP = 4


def flip(position):
    return position + (position // 2) * (1 - 2 * (position % 2))


def where_am_i():
    me = lax.axis_index("seq")
    return me // GROUP, me % GROUP


def device(plane, spot):
    return {"seq": plane * GROUP + spot}


def remote(source, target, sems, index, place):
    return pltpu.make_async_remote_copy(
        src_ref=source, dst_ref=target, send_sem=sems[0].at[index], recv_sem=sems[1].at[index],
        device_id=place, device_id_type=MESH,
    )


def greet(places):
    barrier = pltpu.get_barrier_semaphore()
    for place in places:
        pl.semaphore_signal(barrier, inc=1, device_id=place, device_id_type=MESH)
    pl.semaphore_wait(barrier, len(places))


class Ring:
    def __init__(self, own, slot, sems, base, mine, left, right, left_dev, right_dev):
        self.first = [
            remote(own(0), slot(mine, 0), sems, base, right_dev),
            remote(own(1), slot(mine, 1), sems, base + 1, left_dev),
            remote(own(1), slot(mine, 1), sems, base + 2, right_dev),
            remote(own(0), slot(mine, 0), sems, base + 3, left_dev),
        ]
        self.onward = [
            remote(slot(left, 0), slot(left, 0), sems, base + 4, right_dev),
            remote(slot(right, 1), slot(right, 1), sems, base + 5, left_dev),
        ]

    def start(self):
        for copy in self.first:
            copy.start()

    def relay(self):
        for arrived, onward in zip(self.first[:2], self.onward):
            arrived.wait_recv()
            onward.start()

    def finish(self):
        for copy in self.first[2:] + self.onward:
            copy.wait_recv()
        for copy in self.first + self.onward:
            copy.wait_send()


class Line:
    def __init__(self, own, slot, sems, base, plane, below, above, below_dev, above_dev):
        last = GROUP - 1

        def block(away):
            return slot((plane + away + GROUP) % GROUP)

        self.own, self.sent, self.arriving = [], [], []
        for step in range(last):
            for side, device_on, ahead in ((1, above_dev, plane < last), (-1, below_dev, plane > 0)):
                index = base + step + (0 if side > 0 else last)
                held = plane >= step if side > 0 else plane <= last - step
                due = plane >= step + 1 if side > 0 else plane <= last - step - 1
                out = remote(
                    own if step == 0 else block(-side * step), block(-side * step), sems, index,
                    device_on)
                came = block(-side * (step + 1))
                self.sent.append((ahead & held, out))
                self.arriving.append((due, remote(came, came, sems, index, device_on)))

    def start(self):
        for when, copy in self.sent[:2]:
            pl.when(when)(copy.start)

    def relay(self):
        for (due, arrived), (when, onward) in zip(self.arriving, self.sent[2:]):
            pl.when(due)(arrived.wait_recv)
            pl.when(when)(onward.start)

    def finish(self):
        for due, arrived in self.arriving[len(self.sent) - 2:]:
            pl.when(due)(arrived.wait_recv)
        for when, copy in self.sent:
            pl.when(when)(copy.wait_send)


def rings():
    plane, spot = where_am_i()
    turn = flip(spot)
    left, right = flip((turn + GROUP - 1) % GROUP), flip((turn + 1) % GROUP)
    flat = (spot, left, right, device(plane, left), device(plane, right))
    below, above = (plane + GROUP - 1) % GROUP, (plane + 1) % GROUP
    tall = (plane, below, above, device(below, spot), device(above, spot))
    return plane, spot, flat, tall


def everyone(plane, spot, tall):
    return [device(plane, (spot + step) % GROUP) for step in range(1, GROUP)] + [tall[3], tall[4]]


def swap(piece, slot, sems, base, plane, spot):
    copies = []
    for step in range(1, GROUP):
        peer = (spot + step) % GROUP
        copies.append(remote(piece(peer), slot(spot), sems, base + step - 1, device(plane, peer)))
    return copies


def multiple(value, by):
    return pl.multiple_of(value, by)


def fetch_all(
    tok, pin, pout, key, query, low_all, rows_all, key_all, query_edge,
    tok_all, pin_all, pieces, key_more, partial, inbox, low, send, recv, local,
):
    plane, spot, flat, tall = rings()
    core = lax.axis_index("ch")
    me, count = lax.axis_index("seq"), lax.axis_size("seq")
    sems = (send, recv)
    rows, ranks, width = tok.shape[0], pin.shape[0], pieces.shape[-1]
    margin = query_edge.shape[0]
    after, before = {"seq": (me + 1) % count}, {"seq": (me + count - 1) % count}
    partner = {"ch": 1 - core}
    greet(everyone(plane, spot, tall) + [partner, after, before])

    def columns(s, extent):
        return pl.ds(multiple(s * extent, extent), extent)

    half_tok, half_low = rows // 2, low.shape[0] // 2

    def low_rows(h):
        return pl.ds(multiple(margin + core * low.shape[0] + h * half_low, 16), half_low)

    tails = [
        remote(key.at[pl.ds(rows - margin, margin)], key_more.at[pl.ds(0, margin)], sems, 0, after),
        remote(query.at[pl.ds(rows - margin, margin)], query_edge, sems, 1, after),
    ]
    rank_swap = swap(
        lambda peer: pout.at[:, columns(peer, width)], lambda s: pieces.at[s], sems, 2, plane, spot)
    key_swap = swap(
        lambda peer: key_more.at[:, columns(peer, width)], lambda s: key_all.at[s], sems, 5,
        plane, spot)
    tokens_ring = Ring(
        lambda h: tok.at[pl.ds(h * half_tok, half_tok)],
        lambda s, h: tok_all.at[s, pl.ds(h * half_tok, half_tok)], sems, 8, *flat)
    pin_ring = Line(
        pin, lambda s: pin_all.at[columns(s, ranks)], sems, 14, *tall)
    rows_ring = Line(pieces, lambda s: rows_all.at[:, s], sems, 20, *tall)
    low_ring = Ring(
        lambda h: low.at[pl.ds(h * half_low, half_low)],
        lambda s, h: low_all.at[low_rows(h), columns(s, low.shape[1])], sems, 26, *flat)
    mine = pl.ds(multiple(core * low.shape[0], 16), low.shape[0])
    others = pl.ds(multiple((1 - core) * low.shape[0], 16), low.shape[0])
    sums = remote(partial.at[others], inbox, sems, 32, partner)
    my_low = low_all.at[pl.ds(multiple(margin + core * low.shape[0], 16), low.shape[0])]
    lows = remote(my_low, my_low, sems, 33, partner)
    edge = remote(
        low_all.at[pl.ds(low_all.shape[0] - margin, margin)], low_all.at[pl.ds(0, margin)],
        sems, 34, tall[4])

    pin_ring.start()
    for copy in rank_swap + tails:
        copy.start()
    tokens_ring.start()
    keep = [
        pltpu.make_async_copy(tok, tok_all.at[spot], local.at[0]),
        pltpu.make_async_copy(pin, pin_all.at[columns(plane, ranks)], local.at[1]),
        pltpu.make_async_copy(pout.at[:, columns(spot, width)], pieces.at[spot], local.at[2]),
        pltpu.make_async_copy(key, key_more.at[pl.ds(margin, rows)], local.at[3]),
    ]
    for copy in keep:
        copy.start()
    for copy in keep:
        copy.wait()
    for copy in tails:
        copy.wait_recv()
    pin_ring.relay()
    for copy in rank_swap:
        copy.wait_recv()
    rows_ring.start()
    last = [
        pltpu.make_async_copy(pieces, rows_all.at[:, plane], local.at[4]),
        pltpu.make_async_copy(key_more.at[:, columns(spot, width)], key_all.at[spot], local.at[5]),
    ]
    for copy in last:
        copy.start()
    tokens_ring.relay()
    for copy in key_swap:
        copy.start()
    tokens_ring.finish()
    pin_ring.finish()

    @pl.loop(0, GROUP)
    def _(s):
        partial[pl.ds(multiple(s * rows, rows), rows), :] = lax.dot_general(
            tok_all[s], pin_all[...], (((1,), (1,)), ((), ())),
            preferred_element_type=jnp.float32)

    sums.start()
    sums.wait()
    low[...] = (partial[mine, :] + inbox[...]).astype(low.dtype)
    low_ring.start()
    keep_low = pltpu.make_async_copy(low, my_low.at[:, columns(spot, low.shape[1])], local.at[6])
    keep_low.start()
    low_ring.relay()
    rows_ring.relay()
    low_ring.finish()
    keep_low.wait()
    lows.start()
    lows.wait()
    edge.start()
    for copy in key_swap:
        copy.wait_recv()
    rows_ring.finish()
    edge.wait()
    for copy in rank_swap + key_swap + tails:
        copy.wait_send()
    for copy in last:
        copy.wait()


def share_states(mine, ends, send, recv, local):
    plane, spot = where_am_i()
    peers = [device((plane + step) % GROUP, spot) for step in range(1, GROUP)]
    greet(peers)
    copies = [
        remote(mine, ends.at[plane], (send, recv), index, peer) for index, peer in enumerate(peers)
    ]
    for copy in copies:
        copy.start()
    keep = pltpu.make_async_copy(mine, ends.at[plane], local.at[0])
    keep.start()
    for copy in copies:
        copy.wait()
    keep.wait()


def give_back(mine, out, send, recv, local):
    plane, spot = where_am_i()
    rows, width = out.shape[0], mine.shape[1]
    greet([device(plane, (spot + step) % GROUP) for step in range(1, GROUP)])

    def piece(peer):
        return mine.at[pl.ds(pl.multiple_of(peer * rows, rows), rows)]

    def slot(s):
        return out.at[:, pl.ds(pl.multiple_of(s * width, width), width)]

    moved = swap(piece, slot, (send, recv), 0, plane, spot)
    for copy in moved:
        copy.start()
    keep = pltpu.make_async_copy(piece(spot), slot(spot), local.at[0])
    keep.start()
    for copy in moved:
        copy.wait_recv()
    for copy in moved:
        copy.wait_send()
    keep.wait()


def talk(kernel, shapes, in_specs, scratch, copies, locals_, ident):
    one = not isinstance(shapes, (list, tuple))
    return pl.pallas_call(
        kernel,
        out_shape=shapes,
        in_specs=in_specs,
        out_specs=ANY if one else [ANY] * len(shapes),
        scratch_shapes=scratch + [
            pltpu.SemaphoreType.DMA((copies,)),
            pltpu.SemaphoreType.DMA((copies,)),
            pltpu.SemaphoreType.DMA((locals_,)),
        ],
        compiler_params=pltpu.CompilerParams(collective_id=ident, has_side_effects=True),
    )


def tile_of(source, row, target, place):
    tall, lanes = target.shape[-2:]
    start = where_am_i()[1] * (tall * lanes)
    for column in range(tall):
        cols = pl.ds(pl.multiple_of(start + column * lanes, lanes), lanes)
        target[(*place, pl.ds(column, 1))] = source[(*row, cols)]


def end_states(
    value, key, all_taps, all_rates, spread, states, values, keys, taps, decay
):
    modes, tall, lanes = decay.shape
    for mode in range(modes):
        tile_of(all_rates, (pl.ds(mode, 1),), decay, (mode,))
        decay[mode] = jnp.exp(-decay[mode])
    for branch in range(2):
        for tap in range(taps.shape[1]):
            tile_of(all_taps, (branch + 1, pl.ds(tap, 1)), taps, (branch, tap))
    margin = value.shape[0] - spread.shape[0] // tall
    count, rows = taps.shape[1], spread.shape[0] // tall
    piece = key.shape[1] - margin

    def lay(target, start, load):
        for column in range(tall):
            tile = load(slice(column * lanes, (column + 1) * lanes)).astype(jnp.float32)
            target[pl.ds(start * tall + column, 16, stride=tall), :] = tile

    @pl.loop(0, value.shape[0] // 16)
    def _(block):
        start = pl.multiple_of(block * 16, 16)
        lay(values, start, lambda cols: value[pl.ds(start, 16), cols])

    for edge in range(0, margin, 16):
        lay(keys, edge, lambda cols: key[0, edge:edge + 16, cols])
    for part in range(key.shape[0]):

        @pl.loop(0, piece // 16)
        def _(block):
            start = pl.multiple_of(block * 16, 16)
            lay(keys, margin + part * piece + start,
                lambda cols: key[part, pl.ds(margin + start, 16), cols])

    on = (where_am_i()[0] > 0).astype(jnp.float32)
    for row in range(margin):
        for target in (values, keys):
            place = slice(row * tall, (row + 1) * tall)
            target[place, :] = target[place, :] * on

    rates = [decay[mode] for mode in range(modes)]
    gains = [[taps[branch, tap] for tap in range(count)] for branch in range(2)]

    def short(source, gain, at):
        total = None
        for tap in range(count):
            place = pl.ds(pl.multiple_of((at + margin - tap) * tall, tall), tall)
            term = gain[tap] * source[place, :]
            total = term if total is None else total + term
        return total

    def step(at, held):
        for part in range(4):
            now = at * 4 + part
            mixed = short(keys, gains[0], now) * short(values, gains[1], now)
            mixed = mixed.astype(jnp.bfloat16).astype(jnp.float32)
            spread[pl.ds(pl.multiple_of(now * tall, tall), tall), :] = mixed
            held = [h * r + mixed for h, r in zip(held, rates)]
        return held

    held = lax.fori_loop(0, rows // 4, step, [jnp.zeros((tall, lanes), jnp.float32)] * modes)
    for mode in range(modes):
        states[mode] = held[mode]


def run_states(spread, ends, all_rates, residues, skip, out, kept, rate, weight, gains):
    modes, tall, lanes = rate.shape
    rows = out.shape[0]
    plane = where_am_i()[0]
    for mode in range(modes):
        tile_of(all_rates, (pl.ds(mode, 1),), rate, (mode,))
        tile_of(residues, (pl.ds(mode, 1),), weight, (mode,))
    tile_of(skip, (pl.ds(0, 1),), gains, ())
    rates = [jnp.exp(-rate[mode]) for mode in range(modes)]
    weights = [weight[mode] * jnp.sqrt(rate[mode]) for mode in range(modes)]
    gain = gains[...]

    def step(at, held):
        for part in range(4):
            place = pl.ds(pl.multiple_of((at * 4 + part) * tall, tall), tall)
            value = spread[place, :]
            held = [h * r + value for h, r in zip(held, rates)]
            terms = [h * w for h, w in zip(held, weights)]
            while len(terms) > 1:
                terms = [a + b for a, b in zip(terms[::2], terms[1::2])]
            rounded = terms[0].astype(jnp.bfloat16).astype(jnp.float32)
            kept[place, :] = rounded + gain * value
        return held

    carried = []
    for mode in range(modes):
        total = jnp.zeros((tall, lanes), jnp.float32)
        for at in range(ends.shape[0] - 1):
            longer = total * jnp.exp(-rate[mode] * rows) + ends[at, mode]
            total = jnp.where(at < plane, longer, total)
        carried.append(total)
    lax.fori_loop(0, rows // 4, step, carried)

    @pl.loop(0, rows // 16)
    def _(block):
        start = pl.multiple_of(block * 16, 16)
        for column in range(tall):
            tile = kept[pl.ds(start * tall + column, 16, stride=tall), :]
            out[pl.ds(start, 16), column * lanes:(column + 1) * lanes] = tile.astype(jnp.bfloat16)


def planes_device(
    tokens, query_in, key_in, proj_in, proj_out, short_taps, residues, mode_rates, skip_gain
):
    rows, channels = tokens.shape
    ranks = proj_in.shape[1]
    modes = residues.shape[0]
    margin_rows = short_taps.shape[1] - 1
    width, all_rows = channels // GROUP, rows * GROUP
    tall = width // 128
    half = jnp.bfloat16
    shape = jax.ShapeDtypeStruct
    plane, spot = where_am_i()
    margin = 16
    share, both = GROUP * ranks, GROUP * GROUP * ranks

    low_all, rows_all, key_all, query_edge = talk(
        fetch_all,
        [shape((margin + all_rows, both), half), shape((GROUP, GROUP, ranks, width), half),
         shape((GROUP, margin + rows, width), half), shape((margin, channels), half)],
        [VMEM] * 4 + [ANY],
        [pltpu.VMEM((GROUP, rows, channels), half), pltpu.VMEM((share, channels), half),
         pltpu.VMEM((GROUP, ranks, width), half), pltpu.VMEM((margin + rows, channels), half),
         pltpu.VMEM((all_rows, share), jnp.float32),
         pltpu.VMEM((all_rows // 2, share), jnp.float32), pltpu.VMEM((all_rows // 2, share), half)],
        35, 7, 1,
    )(tokens, proj_in.T, proj_out, key_in, query_in)
    value = jnp.dot(
        low_all, rows_all.reshape(both, width), preferred_element_type=jnp.float32).astype(half)

    tiles, tile = (modes, tall, 128), (tall, 128)
    scattered = pltpu.VMEM(((margin + all_rows) * tall, 128), jnp.float32)
    spread, states = pl.pallas_call(
        end_states,
        out_shape=[shape((all_rows * tall, 128), jnp.float32), shape(tiles, jnp.float32)],
        in_specs=[VMEM] * 4, out_specs=[VMEM] * 2,
        scratch_shapes=[
            scattered, scattered, pltpu.VMEM((2, margin_rows + 1, *tile), jnp.float32),
            pltpu.VMEM(tiles, jnp.float32)],
    )(value, key_all, short_taps, mode_rates)
    ends = talk(share_states, shape((GROUP, *tiles), jnp.float32), [VMEM], [], 3, 1, 2)(states)
    mixed_out = pl.pallas_call(
        run_states,
        out_shape=shape((all_rows, width), half),
        in_specs=[VMEM] * 5, out_specs=VMEM,
        scratch_shapes=[
            pltpu.VMEM((all_rows * tall, 128), jnp.float32), pltpu.VMEM(tiles, jnp.float32),
            pltpu.VMEM(tiles, jnp.float32), pltpu.VMEM(tile, jnp.float32)],
    )(spread, ends, mode_rates, residues, skip_gain[None])
    given = talk(give_back, shape((rows, channels), half), [VMEM], [], 3, 1, 3)(mixed_out)
    first = lax.axis_index("seq") == 0
    query_previous = jnp.where(first, 0, query_edge[margin - margin_rows:]).astype(half)
    query_short = short_filter(query_previous, query_in, short_taps[0])
    return (query_short * given.astype(jnp.float32)).astype(half)


precise = lax.Precision.HIGHEST


def carried_in(value, axis, join, neutral):
    count, mine = (lax.axis_size(axis), lax.axis_index(axis))
    pieces = jax.tree.map(lambda part: lax.all_gather(part, axis), value)
    total = jax.tree.map(
        lambda part, zero: jnp.full_like(part, 0) + jnp.asarray(zero, part.dtype), value, neutral
    )

    def turn(position, total):
        longer = join(total, jax.tree.map(lambda part: part[position], pieces))
        return jax.tree.map(lambda new, old: jnp.where(position < mine, new, old), longer, total)

    return lax.fori_loop(0, count - 1, turn, total)


def passed_along(value, axis, steps):
    count = lax.axis_size(axis)
    leading, last = (max(0, -steps), min(count, count - steps))
    return lax.ppermute(value, axis, [(source, source + steps) for source in range(leading, last)])


def short_filter(previous, current, filter_taps):
    margin_rows = filter_taps.shape[0] - 1
    length = current.shape[0]
    extended = jnp.concatenate([previous, current], axis=0).astype(jnp.float32)
    result = filter_taps[0] * extended[margin_rows : margin_rows + length]
    for offset in range(1, margin_rows + 1):
        result = (
            result
            + filter_taps[offset] * extended[margin_rows - offset : margin_rows - offset + length]
        )
    return result


def carry_states(earlier, later):
    return (earlier[0] * later[1] + later[0], earlier[1] * later[1])


def modal_convolve(mixed, residues, mode_rates):
    tok_rows = mixed.shape[0]
    signal = mixed.astype(jnp.float32)
    steps = jnp.arange(tok_rows, dtype=jnp.int32)
    lower = (steps[:, None] >= steps[None, :]).astype(jnp.float32)
    centred = (steps.astype(jnp.float32) - 0.5 * tok_rows)[:, None]
    local_total = jnp.zeros(signal.shape, jnp.float32)
    end_list = []
    for mode_index in range(residues.shape[0]):
        rate_mode = mode_rates[mode_index]
        weight = residues[mode_index] * jnp.sqrt(rate_mode)
        rising = jnp.exp(rate_mode * centred)
        falling = jnp.exp(-rate_mode * centred)
        running = falling * jnp.dot(lower, rising * signal, precision=precise)
        local_total = local_total + weight * running
        end_list.append(running[tok_rows - 1])
    end_states = jnp.stack(end_list)
    block_decay = jnp.exp(-mode_rates * tok_rows)
    identity = (jnp.zeros(end_states.shape, jnp.float32), jnp.ones(end_states.shape, jnp.float32))
    carried, _ = carried_in((end_states, block_decay), "seq", carry_states, identity)
    after = (steps.astype(jnp.float32) + 1.0)[:, None]
    for mode_index in range(residues.shape[0]):
        rate_mode = mode_rates[mode_index]
        weight = residues[mode_index] * jnp.sqrt(rate_mode)
        local_total = local_total + weight * carried[mode_index] * jnp.exp(-rate_mode * after)
    rounded = lax.optimization_barrier(local_total.astype(jnp.bfloat16))
    return rounded.astype(jnp.float32)


def per_device(
    tokens, query_in, key_in, proj_in, proj_out, short_taps, residues, mode_rates, skip_gain
):
    tok_rows = tokens.shape[0]
    margin_rows = short_taps.shape[1] - 1
    partial_value = jnp.dot(
        tokens,
        lax.all_gather(proj_in, "seq", axis=1, tiled=True),
        preferred_element_type=jnp.float32,
    )
    low_rank = lax.psum(partial_value, "ch").astype(jnp.bfloat16)
    value_full = jnp.dot(
        low_rank,
        lax.all_gather(proj_out, "seq", axis=0, tiled=True),
        preferred_element_type=jnp.float32,
    )
    value_proj = value_full.astype(jnp.bfloat16)
    edges = jnp.stack(
        [
            query_in[tok_rows - margin_rows :],
            key_in[tok_rows - margin_rows :],
            value_proj[tok_rows - margin_rows :],
        ]
    )
    arrived_edges = passed_along(edges, "seq", 1)
    query_previous = arrived_edges[0]
    key_previous = arrived_edges[1]
    value_previous = arrived_edges[2]
    query_short = short_filter(query_previous, query_in, short_taps[0])
    key_short = short_filter(key_previous, key_in, short_taps[1])
    value_short = short_filter(value_previous, value_proj, short_taps[2])
    mixed = (key_short * value_short).astype(jnp.bfloat16)
    convolved_tokens = modal_convolve(mixed, residues, mode_rates)
    return (query_short * (convolved_tokens + skip_gain * mixed.astype(jnp.float32))).astype(
        jnp.bfloat16
    )


def chosen(mesh):
    def run(*args):
        rows, channels = args[0].shape
        ranks = args[3].shape[1]
        square = mesh.shape["seq"] == GROUP * GROUP and mesh.shape["ch"] == 2
        whole = channels % (GROUP * 1024) == 0 and ranks % 32 == 0 and rows % 32 == 0
        fits = (GROUP * ranks) % 128 == 0 and channels == GROUP * 1024
        fits = fits and args[5].shape[1] <= 16
        return (planes_device if square and whole and fits else per_device)(*args)

    return run


def solution(mesh):
    placed = (
        P("seq", "ch"),
        P("seq", "ch"),
        P("seq", "ch"),
        P("ch", "seq"),
        P("seq", "ch"),
        P(None, None, "ch"),
        P(None, "ch"),
        P(None, "ch"),
        P("ch"),
    )
    return jax.shard_map(
        chosen(mesh), mesh=mesh, in_specs=placed, out_specs=P("seq", "ch"), check_vma=False
    )
```

profile of v0, /device:TPU:0, one launch (start us, length us, event | category | flops | bytes accessed | tf_op | source)
XLA Modules:
  0.0 169.6 jit_solution(6662131241462523641)
XLA Ops:
  0.0 120.2 %shard_map.91 = (bf16[528,1536]{1,0:T(8,128)(2,1)}, bf16[4,4,96,1024]{3,2,1,0:T(8,128)(2,1)}, bf16[4,144,1024]{2,1,0:T(8,128)(2,1)}, bf16[16,4096]{1,0:T(8,128)(2,1)}) custom-call(bf16[128,4096]{1,0:T(8,128)(2,1)} %tok.1, bf16[96,4096]{1,0:T(8,128)(2,1)} %bitcast.12, bf16[96,4096]{1,0:T(8,128)(2,1)} %pout.1, bf16[128,4096]{1,0:T(8,128)(2,1)} %key.1, ...), custom_call_target="tpu_custom_call" | custom-call | tf_op jit(solution)/shard_map/pallas_call | solution.py:428
  120.2 5.2 %convolution_convert_fusion.value = bf16[528,1024]{1,0:T(8,128)(2,1)} fusion(bf16[528,1536]{1,0:T(8,128)(2,1)} %get-tuple-element.12, bf16[1536,1024]{1,0:T(8,128)(2,1)} %bitcast.21), kind=kOutput, calls=%fused_computation.15 | convolution fusion | flops 1661485056 | bytes 5849088 | tf_op jit(solution)/shard_map/dot_general | solution.py:439
  125.5 9.7 %shard_map.92 = (f32[4096,128]{1,0:T(8,128)}, f32[16,8,128]{2,1,0:T(8,128)}) custom-call(bf16[528,1024]{1,0:T(8,128)(2,1)} %convolution_convert_fusion.value, bf16[4,144,1024]{2,1,0:T(8,128)(2,1)} %get-tuple-element.14.key, f32[3,7,4096]{2,1,0:T(8,128)} %all_taps.1, f32[16,4096]{1,0:T(8,128)} %all_rates.3), custom_call_target="tpu_custom_call" | custom-call | tf_op jit(solution)/shard_map/pallas_call | solution.py:444
  135.1 8.0 %shard_map.93.ends = f32[4,16,8,128]{3,2,1,0:T(8,128)} custom-call(f32[16,8,128]{2,1,0:T(8,128)} %get-tuple-element.16.mine), custom_call_target="tpu_custom_call" | custom-call | tf_op jit(solution)/shard_map/pallas_call | solution.py:452
  143.1 8.9 %shard_map.94.mine = bf16[512,1024]{1,0:T(8,128)(2,1)} custom-call(f32[4096,128]{1,0:T(8,128)} %get-tuple-element.15.spread, f32[4,16,8,128]{3,2,1,0:T(8,128)} %shard_map.93.ends, f32[16,4096]{1,0:T(8,128)} %all_rates.3, f32[16,4096]{1,0:T(8,128)} %residues.1, f32[1,4096]{1,0:T(1,128)} %bitcast.20), custom_call_target="tpu_custom_call" | custom-call | tf_op jit(solution)/shard_map/pallas_call | solution.py:453
  152.1 0.0 copy-start.2
  152.1 0.0 copy-start.1
  152.1 12.9 %shard_map.95 = bf16[128,4096]{1,0:T(8,128)(2,1)} custom-call(bf16[512,1024]{1,0:T(8,128)(2,1)} %shard_map.94.mine), custom_call_target="tpu_custom_call" | custom-call | tf_op jit(solution)/shard_map/pallas_call | solution.py:461
  165.0 0.0 copy-start
  165.0 1.5 fusion.8
  166.5 0.0 copy-done.2
  166.5 0.0 copy-done.1
  166.5 0.3 maximum_convert_fusion
  166.8 0.0 copy-done
  166.8 2.7 %fusion.2 = bf16[128,4096]{1,0:T(8,128)(2,1)} fusion(f32[134,4096]{1,0:T(8,128)S(1)} %maximum_convert_fusion, bf16[128,4096]{1,0:T(8,128)(2,1)S(1)} %copy-done, f32[4096]{0:T(1024)S(1)} %bitcast.19, f32[4096]{0:T(1024)S(1)} %bitcast.14, f32[4096]{0:T(1024)S(1)} %bitcast.15, f32[4096]{0:T(1024)S(1)} %bitcast.16, f32[4096]{0:T(1024)S(1)} %bitcast.17, ...), kind=kLoop, calls=%fused_computation.3 | loop fusion | flops 8388608 | bytes 16891904 | tf_op jit(solution)/shard_map/convert_element_type | solution.py:465
  (1 shorter events, 0.0 us)
Async XLA Ops:
  152.1 14.4 %copy-start.2 = (bf16[16,4096]{1,0:T(8,128)(2,1)S(1)}, bf16[16,4096]{1,0:T(8,128)(2,1)}, u32[]{:S(2)}) copy-start(bf16[16,4096]{1,0:T(8,128)(2,1)} %get-tuple-element.11) | copy-start | bytes 393220
  152.1 14.5 %copy-start.1 = (bf16[128,4096]{1,0:T(8,128)(2,1)S(1)}, bf16[128,4096]{1,0:T(8,128)(2,1)}, u32[]{:S(2)}) copy-start(bf16[128,4096]{1,0:T(8,128)(2,1)} %query.1) | copy-start | bytes 3145732
  165.0 1.9 %copy-start = (bf16[128,4096]{1,0:T(8,128)(2,1)S(1)}, bf16[128,4096]{1,0:T(8,128)(2,1)}, u32[]{:S(2)}) copy-start(bf16[128,4096]{1,0:T(8,128)(2,1)} %shard_map.95) | copy-start | bytes 3145732
where the time goes:
time: 170 us
  Pallas kernels  160 us (94%)
  matrix products  5.22 us (3%)
  other arithmetic  3.02 us (2%)
    pallas_call x1, Pallas kernels, planes_device(): talk(fetch_all, [shape((margin + all_rows, both), half), shape((GROUP, GR...  120 us
    pallas_call x1, Pallas kernels, planes_device(): talk(give_back, shape((rows, channels), half), [VMEM], [], 3, 1, 3)  12.9 us
    pallas_call x1, Pallas kernels, planes_device(): pl.pallas_call(end_states, out_shape=[shape((all_rows * tall, 128), jnp.f...  9.66 us
    pallas_call x1, Pallas kernels, planes_device(): pl.pallas_call(run_states, out_shape=shape((all_rows, width), half), in_s...  8.93 us
    pallas_call x1, Pallas kernels, planes_device(): talk(share_states, shape((GROUP, *tiles), jnp.float32), [VMEM], [], 3, 1, 2)  8 us
    dot_general x1, matrix products, planes_device(): jnp.dot(low_all, rows_all.reshape(both, width), preferred_element_type=jn...  5.22 us

commit v1 on v0

--- a/solution.py
+++ b/solution.py
@@ -13,10 +13,6 @@
 GROUP = 4
 
 
-def flip(position):
-    return position + (position // 2) * (1 - 2 * (position % 2))
-
-
 def where_am_i():
     me = lax.axis_index("seq")
     return me // GROUP, me % GROUP
@@ -38,85 +34,6 @@
     for place in places:
         pl.semaphore_signal(barrier, inc=1, device_id=place, device_id_type=MESH)
     pl.semaphore_wait(barrier, len(places))
-
-
-class Ring:
-    def __init__(self, own, slot, sems, base, mine, left, right, left_dev, right_dev):
-        self.first = [
-            remote(own(0), slot(mine, 0), sems, base, right_dev),
-            remote(own(1), slot(mine, 1), sems, base + 1, left_dev),
-            remote(own(1), slot(mine, 1), sems, base + 2, right_dev),
-            remote(own(0), slot(mine, 0), sems, base + 3, left_dev),
-        ]
-        self.onward = [
-            remote(slot(left, 0), slot(left, 0), sems, base + 4, right_dev),
-            remote(slot(right, 1), slot(right, 1), sems, base + 5, left_dev),
-        ]
-
-    def start(self):
-        for copy in self.first:
-            copy.start()
-
-    def relay(self):
-        for arrived, onward in zip(self.first[:2], self.onward):
-            arrived.wait_recv()
-            onward.start()
-
-    def finish(self):
-        for copy in self.first[2:] + self.onward:
-            copy.wait_recv()
-        for copy in self.first + self.onward:
-            copy.wait_send()
-
-
-class Line:
-    def __init__(self, own, slot, sems, base, plane, below, above, below_dev, above_dev):
-        last = GROUP - 1
-
-        def block(away):
-            return slot((plane + away + GROUP) % GROUP)
-
-        self.own, self.sent, self.arriving = [], [], []
-        for step in range(last):
-            for side, device_on, ahead in ((1, above_dev, plane < last), (-1, below_dev, plane > 0)):
-                index = base + step + (0 if side > 0 else last)
-                held = plane >= step if side > 0 else plane <= last - step
-                due = plane >= step + 1 if side > 0 else plane <= last - step - 1
-                out = remote(
-                    own if step == 0 else block(-side * step), block(-side * step), sems, index,
-                    device_on)
-                came = block(-side * (step + 1))
-                self.sent.append((ahead & held, out))
-                self.arriving.append((due, remote(came, came, sems, index, device_on)))
-
-    def start(self):
-        for when, copy in self.sent[:2]:
-            pl.when(when)(copy.start)
-
-    def relay(self):
-        for (due, arrived), (when, onward) in zip(self.arriving, self.sent[2:]):
-            pl.when(due)(arrived.wait_recv)
-            pl.when(when)(onward.start)
-
-    def finish(self):
-        for due, arrived in self.arriving[len(self.sent) - 2:]:
-            pl.when(due)(arrived.wait_recv)
-        for when, copy in self.sent:
-            pl.when(when)(copy.wait_send)
-
-
-def rings():
-    plane, spot = where_am_i()
-    turn = flip(spot)
-    left, right = flip((turn + GROUP - 1) % GROUP), flip((turn + 1) % GROUP)
-    flat = (spot, left, right, device(plane, left), device(plane, right))
-    below, above = (plane + GROUP - 1) % GROUP, (plane + 1) % GROUP
-    tall = (plane, below, above, device(below, spot), device(above, spot))
-    return plane, spot, flat, tall
-
-
-def everyone(plane, spot, tall):
-    return [device(plane, (spot + step) % GROUP) for step in range(1, GROUP)] + [tall[3], tall[4]]
 
 
 def swap(piece, slot, sems, base, plane, spot):
@@ -131,114 +48,329 @@
     return pl.multiple_of(value, by)
 
 
+class Place:
+    def __init__(self):
+        self.me, self.core = lax.axis_index("seq"), lax.axis_index("ch")
+        self.count = lax.axis_size("seq")
+        self.plane, self.spot = self.me // GROUP, self.me % GROUP
+        plane, spot = self.plane, self.spot
+        self.side = plane // 2
+        self.outer = (self.side + plane + 1) % 2
+        self.mate, self.cross = plane + 1 - 2 * (plane % 2), 3 - plane
+        self.far = 3 - self.mate
+        self.peers = [spot, spot + 1 - 2 * (spot % 2), (spot + 2) % GROUP, 3 - spot]
+        self.partner = {"ch": 1 - self.core}
+
+    def at_outer(self, run):
+        pl.when(self.outer == 1)(run)
+
+    def at_inner(self, run):
+        pl.when(self.outer == 0)(run)
+
+
+CUTS = 4
+AGAIN = range(1, GROUP)
+W1A, W2A, TOK, KEY = 0, 3, 6, 9
+W1M, W1C, TOKM = 12, 16, 24
+W2M, W2C, W2CM, W2O, W2F = 28, 32, 36, 40, 44
+PAIR, RS, LZ, AG, LD = 48, 52, 64, 66, 72
+EDGE, QT, KT = 80, 81, 82
+COPIES = 83
+
+
 def fetch_all(
-    tok, pin, pout, key, query, low_all, rows_all, key_all, query_edge,
-    tok_all, pin_all, pieces, key_more, partial, inbox, low, send, recv, local,
+    tok, pin, pout, key, query, low_out, rows_out, key_all, query_edge,
+    w1, tok_all, w2, key_more, partial, inbox, summed, parts, mylow, lowout, low_all,
+    send, recv, local,
 ):
-    plane, spot, flat, tall = rings()
-    core = lax.axis_index("ch")
-    me, count = lax.axis_index("seq"), lax.axis_size("seq")
-    sems = (send, recv)
-    rows, ranks, width = tok.shape[0], pin.shape[0], pieces.shape[-1]
-    margin = query_edge.shape[0]
-    after, before = {"seq": (me + 1) % count}, {"seq": (me + count - 1) % count}
-    partner = {"ch": 1 - core}
-    greet(everyone(plane, spot, tall) + [partner, after, before])
-
-    def columns(s, extent):
-        return pl.ds(multiple(s * extent, extent), extent)
-
-    half_tok, half_low = rows // 2, low.shape[0] // 2
-
-    def low_rows(h):
-        return pl.ds(multiple(margin + core * low.shape[0] + h * half_low, 16), half_low)
-
+    p = Place()
+    plane, spot, core, peers = p.plane, p.spot, p.core, p.peers
+    rows, ranks, width = tok.shape[0], pin.shape[0], w2.shape[-1]
+    margin, half = query_edge.shape[0], rows // 2
+    share, both = GROUP * ranks, GROUP * GROUP * ranks
+    wide, sub = both // 2, width // CUTS
+    after = {"seq": (p.me + 1) % p.count}
+    before = {"seq": (p.me + p.count - 1) % p.count}
+
+    barrier = pltpu.get_barrier_semaphore()
+    greeted = [device(plane, peers[k]) for k in AGAIN]
+    greeted += [device(p.mate, spot), p.partner, after, before]
+    for place in greeted:
+        pl.semaphore_signal(barrier, inc=1, device_id=place, device_id_type=MESH)
+
+    @p.at_inner
+    def _():
+        pl.semaphore_signal(barrier, inc=1, device_id=device(p.cross, spot), device_id_type=MESH)
+
+    pl.semaphore_wait(barrier, len(greeted) + 1 - p.outer)
+
+    def go(source, target, index, place):
+        return remote(source, target, (send, recv), index, place)
+
+    def cols(s):
+        return pl.ds(multiple(s * width, width), width)
+
+    def w1_rows(at, s):
+        return pl.ds(multiple((at * GROUP + s) * ranks, ranks), ranks)
+
+    def tok_rows(b, s):
+        return pl.ds(multiple((b * GROUP + s) * rows, rows), rows)
+
+    def cut(c):
+        return slice(c * sub, (c + 1) * sub)
+
+    def halves(h):
+        return pl.ds(multiple(h * wide, wide), wide)
+
+    def low_rows(s, j):
+        return pl.ds(multiple(margin + s * rows + j * half, margin), half)
+
+    def scatter(source, target, base):
+        return [go(source(peers[k]), target, base + k - 1, device(plane, peers[k])) for k in AGAIN]
+
+    mate_dev, cross_dev = device(p.mate, spot), device(p.cross, spot)
+    mine1 = w1.at[w1_rows(plane, spot)]
+    w1_swap = scatter(lambda s: pin.at[:, cols(s)], mine1, W1A)
+    tok_swap = scatter(lambda s: tok.at[:, cols(s)], tok_all.at[tok_rows(p.outer, spot)], TOK)
+    w2_swap = scatter(lambda s: pout.at[:, cols(s)], w2.at[plane, spot], W2A)
+    key_swap = scatter(lambda s: key_more.at[:, cols(s)], key_all.at[spot], KEY)
     tails = [
-        remote(key.at[pl.ds(rows - margin, margin)], key_more.at[pl.ds(0, margin)], sems, 0, after),
-        remote(query.at[pl.ds(rows - margin, margin)], query_edge, sems, 1, after),
+        go(key.at[pl.ds(rows - margin, margin)], key_more.at[pl.ds(0, margin)], KT, after),
+        go(query.at[pl.ds(rows - margin, margin)], query_edge, QT, after),
     ]
-    rank_swap = swap(
-        lambda peer: pout.at[:, columns(peer, width)], lambda s: pieces.at[s], sems, 2, plane, spot)
-    key_swap = swap(
-        lambda peer: key_more.at[:, columns(peer, width)], lambda s: key_all.at[s], sems, 5,
-        plane, spot)
-    tokens_ring = Ring(
-        lambda h: tok.at[pl.ds(h * half_tok, half_tok)],
-        lambda s, h: tok_all.at[s, pl.ds(h * half_tok, half_tok)], sems, 8, *flat)
-    pin_ring = Line(
-        pin, lambda s: pin_all.at[columns(s, ranks)], sems, 14, *tall)
-    rows_ring = Line(pieces, lambda s: rows_all.at[:, s], sems, 20, *tall)
-    low_ring = Ring(
-        lambda h: low.at[pl.ds(h * half_low, half_low)],
-        lambda s, h: low_all.at[low_rows(h), columns(s, low.shape[1])], sems, 26, *flat)
-    mine = pl.ds(multiple(core * low.shape[0], 16), low.shape[0])
-    others = pl.ds(multiple((1 - core) * low.shape[0], 16), low.shape[0])
-    sums = remote(partial.at[others], inbox, sems, 32, partner)
-    my_low = low_all.at[pl.ds(multiple(margin + core * low.shape[0], 16), low.shape[0])]
-    lows = remote(my_low, my_low, sems, 33, partner)
-    edge = remote(
-        low_all.at[pl.ds(low_all.shape[0] - margin, margin)], low_all.at[pl.ds(0, margin)],
-        sems, 34, tall[4])
-
-    pin_ring.start()
-    for copy in rank_swap + tails:
-        copy.start()
-    tokens_ring.start()
+
+    def own_or(first, arrived, k):
+        return first if k == 0 else arrived
+
+    w1_mate = [
+        go(own_or(pin.at[:, cols(spot)], w1.at[w1_rows(plane, peers[k])], k),
+           w1.at[w1_rows(plane, peers[k])], W1M + k, mate_dev) for k in range(GROUP)]
+    w1_cross = [
+        go(own_or(pin.at[:, cols(spot)], w1.at[w1_rows(plane, peers[k])], k),
+           w1.at[w1_rows(plane, peers[k])], W1C + k, cross_dev) for k in range(GROUP)]
+    w1_on = [
+        go(w1.at[w1_rows(p.mate, peers[k])], w1.at[w1_rows(p.mate, peers[k])],
+           W1C + GROUP + k, cross_dev) for k in range(GROUP)]
+    tok_mate = [
+        go(own_or(tok.at[:, cols(spot)], tok_all.at[tok_rows(1, peers[k])], k),
+           tok_all.at[tok_rows(1, peers[k])], TOKM + k, mate_dev) for k in range(GROUP)]
+
+    def strip(at, c, base, place):
+        block = w2.at[at, :, :, cut(c)]
+        return go(block, block, base + c, place)
+
+    every = range(CUTS)
+    w2_mate = [strip(plane, c, W2M, mate_dev) for c in every]
+    w2_cross = [strip(plane, c, W2C, cross_dev) for c in every]
+    w2_on = [strip(p.mate, c, W2CM, cross_dev) for c in every]
+    w2_out = [strip(p.cross, c, W2O, mate_dev) for c in every]
+    w2_far = [strip(p.far, c, W2F, mate_dev) for c in every]
+
+    def low_piece(h):
+        return mylow.at[:, halves(h)]
+
+    sides = [p.side, 1 - p.side]
+
+    def run(copies, what):
+        for copy in copies:
+            getattr(copy, what)()
+
+    run(w1_swap, "start")
+    p.at_outer(w1_mate[0].start)
+    p.at_inner(w1_cross[0].start)
+    run(tails, "start")
+    run(w2_swap, "start")
+    run(tok_swap, "start")
+    w1[w1_rows(plane, spot), :] = pin[:, cols(spot)]
+    tok_all[tok_rows(p.outer, spot), :] = tok[:, cols(spot)]
     keep = [
-        pltpu.make_async_copy(tok, tok_all.at[spot], local.at[0]),
-        pltpu.make_async_copy(pin, pin_all.at[columns(plane, ranks)], local.at[1]),
-        pltpu.make_async_copy(pout.at[:, columns(spot, width)], pieces.at[spot], local.at[2]),
-        pltpu.make_async_copy(key, key_more.at[pl.ds(margin, rows)], local.at[3]),
+        pltpu.make_async_copy(pout.at[:, cols(spot)], w2.at[plane, spot], local.at[0]),
+        pltpu.make_async_copy(key, key_more.at[pl.ds(margin, rows)], local.at[1]),
     ]
-    for copy in keep:
-        copy.start()
-    for copy in keep:
-        copy.wait()
-    for copy in tails:
-        copy.wait_recv()
-    pin_ring.relay()
-    for copy in rank_swap:
-        copy.wait_recv()
-    rows_ring.start()
-    last = [
-        pltpu.make_async_copy(pieces, rows_all.at[:, plane], local.at[4]),
-        pltpu.make_async_copy(key_more.at[:, columns(spot, width)], key_all.at[spot], local.at[5]),
+    run(keep, "start")
+    run(keep, "wait")
+    last = pltpu.make_async_copy(key_more.at[:, cols(spot)], key_all.at[spot], local.at[2])
+
+    def unit(b, h):
+        for n in range(wide // 256):
+            place = pl.ds(multiple(sides[h] * wide + n * 256, 256), 256)
+            found = lax.dot_general(
+                tok_all[b * GROUP * rows:(b + 1) * GROUP * rows, :], w1[place, :],
+                (((1,), (1,)), ((), ())), preferred_element_type=jnp.float32)
+            partial[b, :, :, :, place] = found.reshape(GROUP, 2, half, 256)
+
+    def pair(b, h):
+        return go(partial.at[b, :, 1 - core, :, halves(sides[h])],
+                  inbox.at[b, :, :, halves(sides[h])], PAIR + 2 * b + h, p.partner)
+
+    def reduced(b, h):
+        return [
+            go(summed.at[b, peers[k], :, halves(sides[h])],
+               parts.at[k - 1, b, :, halves(sides[h])], RS + 6 * b + 3 * h + k - 1,
+               device(plane, peers[k])) for k in AGAIN]
+
+    def add_pair(b, h):
+        pair(b, h).wait_recv()
+        place = halves(sides[h])
+        for s in range(GROUP):
+            summed[b, s, :, place] = (
+                partial[b, s, core, :, place] + inbox[b, s, :, place]).astype(summed.dtype)
+        run(reduced(b, h), "start")
+
+    def finish(b, h):
+        run(reduced(b, h), "wait_recv")
+        place = halves(sides[h])
+        total = partial[b, spot, core, :, place] + inbox[b, spot, :, place]
+        for k in AGAIN:
+            total = total + parts[k - 1, b, :, place].astype(jnp.float32)
+        target = lowout if b else mylow
+        target[:, place] = total.astype(target.dtype)
+
+    def low_up(h):
+        return go(lowout.at[:, halves(h)], mylow.at[:, halves(h)], LZ + h, mate_dev)
+
+    def gather(h):
+        return [
+            go(mylow.at[:, halves(h)], low_all.at[low_rows(spot, core), halves(h)],
+               AG + 3 * h + k - 1, device(plane, peers[k])) for k in AGAIN]
+
+    def across(h, k):
+        block = low_all.at[low_rows(peers[k], core), halves(h)]
+        return go(own_or(mylow.at[:, halves(h)], block, k), block, LD + 4 * h + k, p.partner)
+
+    def spread_low(h):
+        run(gather(h), "start")
+        across(h, 0).start()
+        low_all[low_rows(spot, core), halves(h)] = mylow[:, halves(h)]
+
+    @p.at_outer
+    def _():
+        for k in (1, 2, 3):
+            w1_swap[k - 1].wait_recv()
+            w1_mate[k].start()
+        tok_mate[0].start()
+        run(tails, "wait_recv")
+        run(key_swap, "start")
+        last.start()
+        for k in (1, 2, 3):
+            tok_swap[k - 1].wait_recv()
+            tok_mate[k].start()
+        run(w2_swap, "wait_recv")
+        run(w2_mate, "start")
+
+    @p.at_inner
+    def _():
+        def forward(copies, on, which):
+            for k in which:
+                copies[k].wait_recv()
+                on[k].start()
+
+        for k in (1, 2):
+            w1_swap[k - 1].wait_recv()
+            w1_cross[k].start()
+        forward(w1_mate, w1_on, (0,))
+        w1_swap[2].wait_recv()
+        w1_cross[3].start()
+        forward(w1_mate, w1_on, (1, 2, 3))
+        run(w2_swap, "wait_recv")
+        run(w2_mate, "start")
+        run(w2_cross, "start")
+        run(tok_swap, "wait_recv")
+        unit(0, 0)
+        pair(0, 0).start()
+        run(tails, "wait_recv")
+        add_pair(0, 0)
+        run(key_swap, "start")
+        last.start()
+        run(w1_cross + w1_on, "wait_recv")
+        unit(0, 1)
+        pair(0, 1).start()
+        add_pair(0, 1)
+        forward(w2_cross, w2_out, (0,))
+        run(tok_mate, "wait_recv")
+        unit(1, 0)
+        pair(1, 0).start()
+        unit(1, 1)
+        pair(1, 1).start()
+        add_pair(1, 0)
+        forward(w2_cross, w2_out, (1,))
+        add_pair(1, 1)
+        finish(0, 0)
+        finish(0, 1)
+        for h in range(2):
+            spread_low(sides[h])
+        forward(w2_mate, w2_on, (0,))
+        finish(1, 0)
+        low_up(sides[0]).start()
+        forward(w2_cross, w2_out, (2,))
+        finish(1, 1)
+        low_up(sides[1]).start()
+        forward(w2_mate, w2_on, (1,))
+        forward(w2_cross, w2_out, (3,))
+        forward(w2_mate, w2_on, (2, 3))
+
+    @p.at_outer
+    def _():
+        for h in (0, 1):
+            low_up(sides[1 - h]).wait_recv()
+            spread_low(sides[1 - h])
+
+    for h in (0, 1):
+        for k in AGAIN:
+            gather(h)[k - 1].wait_recv()
+            across(h, k).start()
+
+    @p.at_inner
+    def _():
+        for c in every:
+            w2_on[c].wait_recv()
+            w2_far[c].start()
+
+    for h in (0, 1):
+        for k in range(GROUP):
+            across(h, k).wait_recv()
+    above = go(low_all.at[pl.ds(low_all.shape[0] - margin, margin)],
+               low_all.at[pl.ds(0, margin)], EDGE, device((plane + 1) % GROUP, spot))
+    pl.when(plane < GROUP - 1)(above.start)
+
+    @p.at_outer
+    def _():
+        run(w2_mate + w2_out + w2_far, "wait_recv")
+
+    pl.when(plane > 0)(above.wait_recv)
+
+    @pl.when(plane == 0)
+    def _():
+        low_all[0:margin, :] = jnp.zeros((margin, both), low_all.dtype)
+
+    out = [
+        pltpu.make_async_copy(low_all, low_out, local.at[3]),
+        pltpu.make_async_copy(w2, rows_out, local.at[4]),
     ]
-    for copy in last:
-        copy.start()
-    tokens_ring.relay()
-    for copy in key_swap:
-        copy.start()
-    tokens_ring.finish()
-    pin_ring.finish()
-
-    @pl.loop(0, GROUP)
-    def _(s):
-        partial[pl.ds(multiple(s * rows, rows), rows), :] = lax.dot_general(
-            tok_all[s], pin_all[...], (((1,), (1,)), ((), ())),
-            preferred_element_type=jnp.float32)
-
-    sums.start()
-    sums.wait()
-    low[...] = (partial[mine, :] + inbox[...]).astype(low.dtype)
-    low_ring.start()
-    keep_low = pltpu.make_async_copy(low, my_low.at[:, columns(spot, low.shape[1])], local.at[6])
-    keep_low.start()
-    low_ring.relay()
-    rows_ring.relay()
-    low_ring.finish()
-    keep_low.wait()
-    lows.start()
-    lows.wait()
-    edge.start()
-    for copy in key_swap:
-        copy.wait_recv()
-    rows_ring.finish()
-    edge.wait()
-    for copy in rank_swap + key_swap + tails:
-        copy.wait_send()
-    for copy in last:
-        copy.wait()
+    run(out, "start")
+    run(key_swap, "wait_recv")
+    last.wait()
+    run(w1_swap + w2_swap + tok_swap + key_swap + tails, "wait_send")
+    for h in (0, 1):
+        run(gather(h) + [across(h, k) for k in range(GROUP)], "wait_send")
+    pl.when(plane < GROUP - 1)(above.wait_send)
+    run(w2_mate, "wait_send")
+
+    @p.at_outer
+    def _():
+        run(w1_mate + tok_mate, "wait_send")
+
+    @p.at_inner
+    def _():
+        run(w1_cross + w1_on + w2_cross + w2_on + w2_out + w2_far, "wait_send")
+        for b in range(2):
+            for h in range(2):
+                pair(b, h).wait_send()
+                run(reduced(b, h), "wait_send")
+        for h in range(2):
+            low_up(h).wait_send()
+
+    run(out, "wait")
 
 
 def share_states(mine, ends, send, recv, local):
@@ -425,16 +557,19 @@
     margin = 16
     share, both = GROUP * ranks, GROUP * GROUP * ranks
 
+    full, band = jnp.float32, rows // 2
     low_all, rows_all, key_all, query_edge = talk(
         fetch_all,
         [shape((margin + all_rows, both), half), shape((GROUP, GROUP, ranks, width), half),
          shape((GROUP, margin + rows, width), half), shape((margin, channels), half)],
-        [VMEM] * 4 + [ANY],
-        [pltpu.VMEM((GROUP, rows, channels), half), pltpu.VMEM((share, channels), half),
-         pltpu.VMEM((GROUP, ranks, width), half), pltpu.VMEM((margin + rows, channels), half),
-         pltpu.VMEM((all_rows, share), jnp.float32),
-         pltpu.VMEM((all_rows // 2, share), jnp.float32), pltpu.VMEM((all_rows // 2, share), half)],
-        35, 7, 1,
+        [VMEM] * 5,
+        [pltpu.VMEM((both, width), half), pltpu.VMEM((2 * all_rows, width), half),
+         pltpu.VMEM((GROUP, GROUP, ranks, width), half), pltpu.VMEM((margin + rows, channels), half),
+         pltpu.VMEM((2, GROUP, 2, band, both), full), pltpu.VMEM((2, GROUP, band, both), full),
+         pltpu.VMEM((2, GROUP, band, both), half), pltpu.VMEM((GROUP - 1, 2, band, both), half),
+         pltpu.VMEM((band, both), half), pltpu.VMEM((band, both), half),
+         pltpu.VMEM((margin + all_rows, both), half)],
+        COPIES, 7, 5,
     )(tokens, proj_in.T, proj_out, key_in, query_in)
     value = jnp.dot(
         low_all, rows_all.reshape(both, width), preferred_element_type=jnp.float32).astype(half)

time: 170 us -> 162 us (0.953)
  Pallas kernels: 160 us -> 152 us
    pallas_call x1, Pallas kernels: 120 us -> 108 us  [planes_device(): talk(fetch_all, [shape((margin + all_rows, both), half), shape((GROUP, GR...]
    pallas_call x1, Pallas kernels: 12.9 us -> 15.4 us  [planes_device(): talk(give_back, shape((rows, channels), half), [VMEM], [], 3, 1, 3)]
    pallas_call x1, Pallas kernels: 8 us -> 9.81 us  [planes_device(): talk(share_states, shape((GROUP, *tiles), jnp.float32), [VMEM], [], 3, 1, 2)]
where the time goes in v1:
time: 162 us; the launch traced here: 161 us
  Pallas kernels  152 us (94%)
  matrix products  5.22 us (3%)
  other arithmetic  3.02 us (2%)
    pallas_call x1, Pallas kernels, planes_device(): talk(fetch_all, [shape((margin + all_rows, both), half), shape((GROUP, GR...  108 us
    pallas_call x1, Pallas kernels, planes_device(): talk(give_back, shape((rows, channels), half), [VMEM], [], 3, 1, 3)  15.4 us
    pallas_call x1, Pallas kernels, planes_device(): talk(share_states, shape((GROUP, *tiles), jnp.float32), [VMEM], [], 3, 1, 2)  9.81 us
    pallas_call x1, Pallas kernels, planes_device(): pl.pallas_call(end_states, out_shape=[shape((all_rows * tall, 128), jnp.f...  9.66 us
    pallas_call x1, Pallas kernels, planes_device(): pl.pallas_call(run_states, out_shape=shape((all_rows, width), half), in_s...  8.93 us
    dot_general x1, matrix products, planes_device(): jnp.dot(low_all, rows_all.reshape(both, width), preferred_element_type=jn...  5.22 us

profile of v1, /device:TPU:0, one launch (start us, length us, event | category | flops | bytes accessed | tf_op | source)
XLA Modules:
  0.0 161.4 jit_solution(16143256678686047999)
XLA Ops:
  0.0 107.7 %shard_map.91 = (bf16[528,1536]{1,0:T(8,128)(2,1)}, bf16[4,4,96,1024]{3,2,1,0:T(8,128)(2,1)}, bf16[4,144,1024]{2,1,0:T(8,128)(2,1)}, bf16[16,4096]{1,0:T(8,128)(2,1)}) custom-call(bf16[128,4096]{1,0:T(8,128)(2,1)} %tok.1, bf16[96,4096]{1,0:T(8,128)(2,1)} %bitcast.12, bf16[96,4096]{1,0:T(8,128)(2,1)} %pout.1, bf16[128,4096]{1,0:T(8,128)(2,1)} %key.1, ...), custom_call_target="tpu_custom_call" | custom-call | tf_op jit(solution)/shard_map/pallas_call | solution.py:561
  107.8 5.2 %convolution_convert_fusion.value = bf16[528,1024]{1,0:T(8,128)(2,1)} fusion(bf16[528,1536]{1,0:T(8,128)(2,1)} %get-tuple-element.12, bf16[1536,1024]{1,0:T(8,128)(2,1)} %bitcast.21), kind=kOutput, calls=%fused_computation.15 | convolution fusion | flops 1661485056 | bytes 5849088 | tf_op jit(solution)/shard_map/dot_general | solution.py:574
  113.0 9.7 %shard_map.92 = (f32[4096,128]{1,0:T(8,128)}, f32[16,8,128]{2,1,0:T(8,128)}) custom-call(bf16[528,1024]{1,0:T(8,128)(2,1)} %convolution_convert_fusion.value, bf16[4,144,1024]{2,1,0:T(8,128)(2,1)} %get-tuple-element.14.key, f32[3,7,4096]{2,1,0:T(8,128)} %all_taps.1, f32[16,4096]{1,0:T(8,128)} %all_rates.3), custom_call_target="tpu_custom_call" | custom-call | tf_op jit(solution)/shard_map/pallas_call | solution.py:579
  122.6 9.8 %shard_map.93.ends = f32[4,16,8,128]{3,2,1,0:T(8,128)} custom-call(f32[16,8,128]{2,1,0:T(8,128)} %get-tuple-element.16.mine), custom_call_target="tpu_custom_call" | custom-call | tf_op jit(solution)/shard_map/pallas_call | solution.py:587
  132.5 8.9 %shard_map.94.mine = bf16[512,1024]{1,0:T(8,128)(2,1)} custom-call(f32[4096,128]{1,0:T(8,128)} %get-tuple-element.15.spread, f32[4,16,8,128]{3,2,1,0:T(8,128)} %shard_map.93.ends, f32[16,4096]{1,0:T(8,128)} %all_rates.3, f32[16,4096]{1,0:T(8,128)} %residues.1, f32[1,4096]{1,0:T(1,128)} %bitcast.20), custom_call_target="tpu_custom_call" | custom-call | tf_op jit(solution)/shard_map/pallas_call | solution.py:588
  141.4 0.0 copy-start.2
  141.4 0.0 copy-start.1
  141.4 15.4 %shard_map.95 = bf16[128,4096]{1,0:T(8,128)(2,1)} custom-call(bf16[512,1024]{1,0:T(8,128)(2,1)} %shard_map.94.mine), custom_call_target="tpu_custom_call" | custom-call | tf_op jit(solution)/shard_map/pallas_call | solution.py:596
  156.8 0.0 copy-start
  156.8 1.5 fusion.8
  158.4 0.0 copy-done.2
  158.4 0.0 copy-done.1
  158.4 0.3 maximum_convert_fusion
  158.7 0.0 copy-done
  158.7 2.7 %fusion.2 = bf16[128,4096]{1,0:T(8,128)(2,1)} fusion(f32[134,4096]{1,0:T(8,128)S(1)} %maximum_convert_fusion, bf16[128,4096]{1,0:T(8,128)(2,1)S(1)} %copy-done, f32[4096]{0:T(1024)S(1)} %bitcast.19, f32[4096]{0:T(1024)S(1)} %bitcast.14, f32[4096]{0:T(1024)S(1)} %bitcast.15, f32[4096]{0:T(1024)S(1)} %bitcast.16, f32[4096]{0:T(1024)S(1)} %bitcast.17, ...), kind=kLoop, calls=%fused_computation.3 | loop fusion | flops 8388608 | bytes 16891904 | tf_op jit(solution)/shard_map/convert_element_type | solution.py:600
  (1 shorter events, 0.0 us)
Async XLA Ops:
  141.4 17.0 %copy-start.2 = (bf16[16,4096]{1,0:T(8,128)(2,1)S(1)}, bf16[16,4096]{1,0:T(8,128)(2,1)}, u32[]{:S(2)}) copy-start(bf16[16,4096]{1,0:T(8,128)(2,1)} %get-tuple-element.11) | copy-start | bytes 393220
  141.4 17.0 %copy-start.1 = (bf16[128,4096]{1,0:T(8,128)(2,1)S(1)}, bf16[128,4096]{1,0:T(8,128)(2,1)}, u32[]{:S(2)}) copy-start(bf16[128,4096]{1,0:T(8,128)(2,1)} %query.1) | copy-start | bytes 3145732
  156.8 1.9 %copy-start = (bf16[128,4096]{1,0:T(8,128)(2,1)S(1)}, bf16[128,4096]{1,0:T(8,128)(2,1)}, u32[]{:S(2)}) copy-start(bf16[128,4096]{1,0:T(8,128)(2,1)} %shard_map.95) | copy-start | bytes 3145732

commit v2 on v1

v2 whole, which is shorter than its diff:
```python
import functools

import jax
import jax.numpy as jnp
from jax import lax
from jax.experimental import pallas as pl
from jax.experimental.pallas import tpu as pltpu
from jax.sharding import PartitionSpec as P

MESH = pl.DeviceIdType.MESH
VMEM = pl.BlockSpec(memory_space=pltpu.VMEM)
ANY = pl.BlockSpec(memory_space=pl.ANY)
GROUP = 4


def where_am_i():
    me = lax.axis_index("seq")
    return me // GROUP, me % GROUP


def device(plane, spot):
    return {"seq": plane * GROUP + spot}


def remote(source, target, sems, index, place):
    return pltpu.make_async_remote_copy(
        src_ref=source, dst_ref=target, send_sem=sems[0].at[index], recv_sem=sems[1].at[index],
        device_id=place, device_id_type=MESH,
    )


def greet(places):
    barrier = pltpu.get_barrier_semaphore()
    for place in places:
        pl.semaphore_signal(barrier, inc=1, device_id=place, device_id_type=MESH)
    pl.semaphore_wait(barrier, len(places))


def multiple(value, by):
    return pl.multiple_of(value, by)


class Place:
    def __init__(self):
        self.me, self.core = lax.axis_index("seq"), lax.axis_index("ch")
        self.count = lax.axis_size("seq")
        self.plane, self.spot = self.me // GROUP, self.me % GROUP
        plane, spot = self.plane, self.spot
        self.side = plane // 2
        self.outer = (self.side + plane + 1) % 2
        self.mate, self.cross = plane + 1 - 2 * (plane % 2), 3 - plane
        self.far = 3 - self.mate
        self.peers = [spot, spot + 1 - 2 * (spot % 2), (spot + 2) % GROUP, 3 - spot]
        self.partner = {"ch": 1 - self.core}

    def at_outer(self, run):
        pl.when(self.outer == 1)(run)

    def at_inner(self, run):
        pl.when(self.outer == 0)(run)


CUTS = 4
AGAIN = range(1, GROUP)
W1A, W2A, TOK, KEY = 0, 3, 6, 9
W1M, W1C, TOKM = 12, 16, 24
W2M, W2C, W2CM, W2O, W2F = 28, 32, 36, 40, 44
PAIR, RS, LZ, AG, LD = 48, 56, 72, 74, 80
EDGE, QT, KT, KM = 88, 89, 90, 91
COPIES = 94


def fetch_all(
    tok, pin, pout, key, query, low_out, rows_out, key_out, query_edge,
    w1, tok_all, w2, key_all, key_edge, partial, inbox, summed, parts, mylow, lowout, low_all,
    send, recv, local,
):
    p = Place()
    plane, spot, core, peers = p.plane, p.spot, p.core, p.peers
    rows, ranks, width = tok.shape[0], pin.shape[0], w2.shape[-1]
    margin, half = query_edge.shape[0], rows // 2
    share, both = GROUP * ranks, GROUP * GROUP * ranks
    wide, sub = both // 2, width // CUTS
    after = {"seq": (p.me + 1) % p.count}
    before = {"seq": (p.me + p.count - 1) % p.count}

    barrier = pltpu.get_barrier_semaphore()
    greeted = [device(plane, peers[k]) for k in AGAIN]
    greeted += [device(p.mate, spot), p.partner, after, before]
    for place in greeted:
        pl.semaphore_signal(barrier, inc=1, device_id=place, device_id_type=MESH)

    @p.at_inner
    def _():
        pl.semaphore_signal(barrier, inc=1, device_id=device(p.cross, spot), device_id_type=MESH)

    pl.semaphore_wait(barrier, len(greeted) + 1 - p.outer)

    def go(source, target, index, place):
        return remote(source, target, (send, recv), index, place)

    def cols(s):
        return pl.ds(multiple(s * width, width), width)

    def w1_rows(at, s):
        return pl.ds(multiple((at * GROUP + s) * ranks, ranks), ranks)

    def tok_rows(b, s):
        return pl.ds(multiple((b * GROUP + s) * rows, rows), rows)

    def cut(c):
        return slice(c * sub, (c + 1) * sub)

    def halves(h):
        return pl.ds(multiple(h * wide, wide), wide)

    def low_rows(s, j):
        return pl.ds(multiple(margin + s * rows + j * half, margin), half)

    def scatter(source, target, base):
        return [go(source(peers[k]), target, base + k - 1, device(plane, peers[k])) for k in AGAIN]

    mate_dev, cross_dev = device(p.mate, spot), device(p.cross, spot)
    mine1 = w1.at[w1_rows(plane, spot)]
    w1_swap = scatter(lambda s: pin.at[:, cols(s)], mine1, W1A)
    tok_swap = scatter(lambda s: tok.at[:, cols(s)], tok_all.at[tok_rows(p.outer, spot)], TOK)
    w2_swap = scatter(lambda s: pout.at[:, cols(s)], w2.at[plane, spot], W2A)
    key_rows = pl.ds(multiple(margin + spot * rows, margin), rows)
    key_swap = scatter(lambda s: key.at[:, cols(s)], key_all.at[key_rows], KEY)
    tails = [
        go(key.at[pl.ds(rows - margin, margin)], key_edge, KT, after),
        go(query.at[pl.ds(rows - margin, margin)], query_edge, QT, after),
    ]

    def key_margin(k):
        return go(key_edge.at[:, cols(peers[k])], key_all.at[pl.ds(0, margin)], KM + k - 1,
                  device(plane, peers[k]))

    def start_tails():
        run(tails, "start")

    def share_tails():
        @pl.when(p.me > 0)
        def _():
            run(tails, "wait_recv")

        @pl.when((spot == 0) & (plane > 0))
        def _():
            for k in AGAIN:
                key_margin(k).start()
            key_all[0:margin, :] = key_edge[:, cols(spot)]

        run(key_swap, "start")

        @pl.when(plane == 0)
        def _():
            key_all[0:margin, :] = jnp.zeros((margin, width), key_all.dtype)

    def end_tails():
        run(key_swap, "wait_recv")
        for k in AGAIN:
            pl.when((spot == k) & (plane > 0))(key_margin(k).wait_recv)

        @pl.when((spot == 0) & (plane > 0))
        def _():
            for k in AGAIN:
                key_margin(k).wait_send()

        @pl.when(p.me < p.count - 1)
        def _():
            run(tails, "wait_send")

    def own_or(first, arrived, k):
        return first if k == 0 else arrived

    w1_mate = [
        go(own_or(pin.at[:, cols(spot)], w1.at[w1_rows(plane, peers[k])], k),
           w1.at[w1_rows(plane, peers[k])], W1M + k, mate_dev) for k in range(GROUP)]
    w1_cross = [
        go(own_or(pin.at[:, cols(spot)], w1.at[w1_rows(plane, peers[k])], k),
           w1.at[w1_rows(plane, peers[k])], W1C + k, cross_dev) for k in range(GROUP)]
    w1_on = [
        go(w1.at[w1_rows(p.mate, peers[k])], w1.at[w1_rows(p.mate, peers[k])],
           W1C + GROUP + k, cross_dev) for k in range(GROUP)]
    tok_mate = [
        go(own_or(tok.at[:, cols(spot)], tok_all.at[tok_rows(1, peers[k])], k),
           tok_all.at[tok_rows(1, peers[k])], TOKM + k, mate_dev) for k in range(GROUP)]

    def strip(at, c, base, place):
        block = w2.at[at, :, :, cut(c)]
        return go(block, block, base + c, place)

    every = range(CUTS)
    w2_mate = [strip(plane, c, W2M, mate_dev) for c in every]
    w2_cross = [strip(plane, c, W2C, cross_dev) for c in every]
    w2_on = [strip(p.mate, c, W2CM, cross_dev) for c in every]
    w2_out = [strip(p.cross, c, W2O, mate_dev) for c in every]
    w2_far = [strip(p.far, c, W2F, mate_dev) for c in every]

    def run(copies, what):
        for copy in copies:
            getattr(copy, what)()

    run(w1_swap, "start")
    p.at_outer(w1_mate[0].start)
    p.at_outer(tok_mate[0].start)
    p.at_inner(w1_cross[0].start)
    run(tok_swap, "start")
    run(w2_swap, "start")
    pl.when(p.me < p.count - 1)(start_tails)
    w1[w1_rows(plane, spot), :] = pin[:, cols(spot)]
    tok_all[tok_rows(p.outer, spot), :] = tok[:, cols(spot)]
    keep = [
        pltpu.make_async_copy(pout.at[:, cols(spot)], w2.at[plane, spot], local.at[0]),
        pltpu.make_async_copy(key.at[:, cols(spot)], key_all.at[key_rows], local.at[1]),
    ]
    run(keep, "start")
    run(keep, "wait")

    order = [plane, p.cross, p.mate, p.far]

    def quarter(q):
        return pl.ds(multiple(order[q] * share, share), share)

    def multiply(left, place):
        return lax.dot_general(
            left, w1[place, :], (((1,), (1,)), ((), ())), preferred_element_type=jnp.float32)

    def pair(u):
        if u < GROUP:
            source = partial.at[0, :, 1 - core, :, quarter(u)]
            target = inbox.at[0, :, :, quarter(u)]
        else:
            spot_at = peers[u - GROUP]
            source, target = partial.at[1, spot_at, 1 - core], inbox.at[1, spot_at]
        return go(source, target, PAIR + u, p.partner)

    def unit(q):
        found = multiply(tok_all[0:GROUP * rows, :], quarter(q))
        partial[0, :, :, :, quarter(q)] = found.reshape(GROUP, 2, half, share)
        pair(q).start()

    def row_unit(k):
        left = tok_all[tok_rows(1, peers[k]), :]
        for n in range(both // 256):
            found = multiply(left, slice(n * 256, (n + 1) * 256))
            partial[1, peers[k], :, :, n * 256:(n + 1) * 256] = found.reshape(2, half, 256)
        pair(GROUP + k).start()

    def reduced(q):
        return [
            go(summed.at[0, peers[k], :, quarter(q)], parts.at[k - 1, 0, :, quarter(q)],
               RS + 3 * q + k - 1, device(plane, peers[k])) for k in AGAIN]

    def row_reduced(k):
        return go(summed.at[1, peers[k]], parts.at[k - 1, 1], RS + 11 + k, device(plane, peers[k]))

    def add_pair(q):
        pair(q).wait_recv()
        place = quarter(q)
        for s in range(GROUP):
            summed[0, s, :, place] = (
                partial[0, s, core, :, place] + inbox[0, s, :, place]).astype(summed.dtype)
        run(reduced(q), "start")

    def row_add(k):
        pair(GROUP + k).wait_recv()
        if k:
            at = peers[k]
            summed[1, at] = (partial[1, at, core] + inbox[1, at]).astype(summed.dtype)
            row_reduced(k).start()

    def finish(b):
        if b:
            run([row_reduced(k) for k in AGAIN], "wait_recv")
        else:
            for q in range(GROUP):
                run(reduced(q), "wait_recv")
        total = partial[b, spot, core] + inbox[b, spot]
        for k in AGAIN:
            total = total + parts[k - 1, b].astype(jnp.float32)
        target = lowout if b else mylow
        target[...] = total.astype(target.dtype)

    def low_up(h):
        return go(lowout.at[:, halves(h)], mylow.at[:, halves(h)], LZ + h, mate_dev)

    def gather(h):
        return [
            go(mylow.at[:, halves(h)], low_all.at[low_rows(spot, core), halves(h)],
               AG + 3 * h + k - 1, device(plane, peers[k])) for k in AGAIN]

    def across(h, k):
        block = low_all.at[low_rows(peers[k], core), halves(h)]
        return go(own_or(mylow.at[:, halves(h)], block, k), block, LD + 4 * h + k, p.partner)

    def spread_low(h):
        run(gather(h), "start")
        across(h, 0).start()
        low_all[low_rows(spot, core), halves(h)] = mylow[:, halves(h)]

    @p.at_outer
    def _():
        for k in (1, 2):
            w1_swap[k - 1].wait_recv()
            w1_mate[k].start()
        tok_swap[0].wait_recv()
        tok_mate[1].start()
        w1_swap[2].wait_recv()
        w1_mate[3].start()
        for k in (2, 3):
            tok_swap[k - 1].wait_recv()
            tok_mate[k].start()
        run(w2_swap, "wait_recv")
        run(w2_mate, "start")
        share_tails()

    @p.at_inner
    def _():
        def forward(copies, on, which):
            for k in which:
                copies[k].wait_recv()
                on[k].start()

        for k in (1, 2):
            w1_swap[k - 1].wait_recv()
            w1_cross[k].start()
        forward(w1_mate, w1_on, (0,))
        w1_swap[2].wait_recv()
        w1_cross[3].start()
        forward(w1_mate, w1_on, (1, 2))
        run(tok_swap, "wait_recv")
        unit(0)
        run(w1_cross, "wait_recv")
        unit(1)
        add_pair(0)
        add_pair(1)
        forward(w1_mate, w1_on, (3,))
        unit(2)
        run(w2_swap, "wait_recv")
        run(w2_cross, "start")
        run(w2_mate, "start")
        add_pair(2)
        run(w1_on, "wait_recv")
        unit(3)
        tok_mate[0].wait_recv()
        row_unit(0)
        add_pair(3)
        tok_mate[1].wait_recv()
        row_unit(1)
        row_add(0)
        tok_mate[2].wait_recv()
        row_unit(2)
        row_add(1)
        tok_mate[3].wait_recv()
        row_unit(3)
        row_add(2)
        row_add(3)
        forward(w2_cross, w2_out, (0,))
        finish(0)
        for h in range(2):
            spread_low(h)
        forward(w2_cross, w2_out, (1,))
        forward(w2_mate, w2_on, (0,))
        finish(1)
        for h in range(2):
            low_up(h).start()
        share_tails()
        forward(w2_cross, w2_out, (2,))
        forward(w2_mate, w2_on, (1,))
        forward(w2_cross, w2_out, (3,))
        forward(w2_mate, w2_on, (2, 3))

    @p.at_outer
    def _():
        for h in (0, 1):
            low_up(h).wait_recv()
            spread_low(h)

    for h in (0, 1):
        for k in AGAIN:
            gather(h)[k - 1].wait_recv()
            across(h, k).start()

    @p.at_inner
    def _():
        for c in every:
            w2_on[c].wait_recv()
            w2_far[c].start()

    for h in (0, 1):
        for k in range(GROUP):
            across(h, k).wait_recv()
    above = go(low_all.at[pl.ds(low_all.shape[0] - margin, margin)],
               low_all.at[pl.ds(0, margin)], EDGE, device((plane + 1) % GROUP, spot))
    pl.when(plane < GROUP - 1)(above.start)

    @p.at_outer
    def _():
        run(w2_mate + w2_out + w2_far, "wait_recv")

    pl.when(plane > 0)(above.wait_recv)

    @pl.when(plane == 0)
    def _():
        low_all[0:margin, :] = jnp.zeros((margin, both), low_all.dtype)

    end_tails()
    out = [
        pltpu.make_async_copy(key_all, key_out, local.at[2]),
        pltpu.make_async_copy(low_all, low_out, local.at[3]),
        pltpu.make_async_copy(w2, rows_out, local.at[4]),
    ]
    run(out, "start")
    run(w1_swap + w2_swap + tok_swap + key_swap, "wait_send")
    for h in (0, 1):
        run(gather(h) + [across(h, k) for k in range(GROUP)], "wait_send")
    pl.when(plane < GROUP - 1)(above.wait_send)
    run(w2_mate, "wait_send")

    @p.at_outer
    def _():
        run(w1_mate + tok_mate, "wait_send")

    @p.at_inner
    def _():
        run(w1_cross + w1_on + w2_cross + w2_on + w2_out + w2_far, "wait_send")
        for u in range(2 * GROUP):
            pair(u).wait_send()
        for u in range(GROUP):
            run(reduced(u), "wait_send")
        for k in AGAIN:
            row_reduced(k).wait_send()
        for h in range(2):
            low_up(h).wait_send()

    run(out, "wait")


SEGMENTS = 8
LANES = 128
ENDS, GIVE = 0, 24
TAIL_COPIES = 36


def one_hot(rows, columns, target):
    row = lax.broadcasted_iota(jnp.int32, (rows, columns), 0)
    column = lax.broadcasted_iota(jnp.int32, (rows, columns), 1)
    return (column == target(row)).astype(jnp.bfloat16)


def convolve(
    low_all, w2, key_all, query, query_edge, taps, residues, rates, skip, out,
    low_mixed, keys, values, mixed, kept, turned, given, gains, decay, weight, direct, longer,
    states, mine, ends, send, recv,
):
    p = Place()
    plane, spot, peers = p.plane, p.spot, p.peers
    f32, bf16 = jnp.float32, jnp.bfloat16
    margin, rows = query_edge.shape[0], query.shape[0]
    modes, width = decay.shape[0], values.shape[1]
    count = taps.shape[1]
    all_rows = rows * GROUP
    steps = all_rows // SEGMENTS
    lead = SEGMENTS
    spread_rows = (steps + lead) * SEGMENTS
    strip = width // CUTS
    tiles = width // LANES
    both = low_all.shape[1]

    barrier = pltpu.get_barrier_semaphore()
    greeted = [device(plane, peers[k]) for k in AGAIN]
    greeted += [device((plane + d) % GROUP, spot) for d in AGAIN]
    for place in greeted:
        pl.semaphore_signal(barrier, inc=1, device_id=place, device_id_type=MESH)
    pl.semaphore_wait(barrier, len(greeted))

    def go(source, target, index, place):
        return remote(source, target, (send, recv), index, place)

    spread = one_hot(
        spread_rows, margin + all_rows,
        lambda row: margin - lead + steps * (row % SEGMENTS) + row // SEGMENTS)
    gather = one_hot(
        all_rows, all_rows, lambda row: SEGMENTS * (row % steps) + row // steps)

    def dot(left, right):
        return jnp.dot(left, right, preferred_element_type=f32)

    for n in range(both // 256):
        at = slice(n * 256, (n + 1) * 256)
        low_mixed[:, at] = dot(spread, low_all[:, at]).astype(bf16)
    for c in range(CUTS):
        at = slice(c * strip, (c + 1) * strip)
        keys[:, at] = dot(spread, key_all[:, at])
    own = pl.ds(multiple(spot * width, width), width)

    def rows_of(vector):
        return jnp.broadcast_to(vector, (SEGMENTS, width))

    for branch in range(2):
        for tap in range(count):
            gains[branch, tap] = rows_of(taps[branch + 1, pl.ds(tap, 1), own])
    for mode in range(modes):
        rate = rows_of(rates[pl.ds(mode, 1), own])
        decay[mode] = jnp.exp(-rate)
        longer[mode] = rate
        weight[mode] = rows_of(residues[pl.ds(mode, 1), own]) * jnp.sqrt(rate)
    direct[...] = rows_of(skip[pl.ds(0, 1), own])

    for c in range(CUTS):
        at = slice(c * strip, (c + 1) * strip)
        found = dot(low_mixed[...], w2[:, :, :, at].reshape(both, strip))
        values[:, at] = found.astype(bf16).astype(f32)

    def lane(tile):
        return pl.ds(multiple(tile * LANES, LANES), LANES)

    def at_step(j):
        return pl.ds(multiple(j * SEGMENTS, SEGMENTS), SEGMENTS)

    sub = lax.broadcasted_iota(jnp.int32, (SEGMENTS, LANES), 0)

    def down(value, by):
        return jnp.where(sub >= by, pltpu.roll(value, by, 0), 0.0)

    def mix(tile):
        cols = lane(tile)
        tap = [[gains[b, t, :, cols] for t in range(count)] for b in range(2)]

        def filtered(source, b, j):
            total = None
            for t in range(count):
                term = tap[b][t] * source[at_step(j + lead - t), cols]
                total = term if total is None else total + term
            return total

        @pl.loop(0, steps // 8)
        def _(block):
            for part in range(8):
                j = block * 8 + part
                product = filtered(keys, 0, j) * filtered(values, 1, j)
                mixed[at_step(j), cols] = product.astype(bf16).astype(f32)

    def end_of(tile):
        cols = lane(tile)
        factor = [decay[n, :, cols] for n in range(modes)]

        def body(block, held):
            for part in range(8):
                value = mixed[at_step(block * 8 + part), cols]
                held = [h * r + value for h, r in zip(held, factor)]
            return held

        held = lax.fori_loop(0, steps // 8, body, [jnp.zeros((SEGMENTS, LANES), f32)] * modes)
        for n in range(modes):
            rate = longer[n, :, cols]
            total = held[n]
            for power in (1, 2, 4):
                total = total + jnp.exp(-rate * (steps * power)) * down(total, power)
            states[n, :, cols] = down(total, 1)
            mine[tile, pl.ds(n, 1), :] = total[SEGMENTS - 1:, :]

    def ends_copy(tile, d):
        return go(mine.at[tile], ends.at[tile, d - 1], ENDS + tile * 3 + d - 1,
                  device((plane + d) % GROUP, spot))

    def share(tile):
        for d in AGAIN:
            pl.when(plane + d < GROUP)(ends_copy(tile, d).start)

    def arrive(tile):
        for d in AGAIN:
            pl.when(plane >= d)(ends_copy(tile, d).wait_recv)

    def conv(tile):
        cols = lane(tile)
        factor = [decay[n, :, cols] for n in range(modes)]
        start = []
        for n in range(modes):
            rate = longer[n, :, cols]
            row = rate[0:1]
            total = jnp.zeros((1, LANES), f32)
            for d in reversed(AGAIN):
                far = jnp.exp(-row * (all_rows * (d - 1))) * ends[tile, d - 1, pl.ds(n, 1), :]
                total = jnp.where(plane >= d, total + far, total)
            spent = jnp.exp(-rate * (steps * sub.astype(f32)))
            start.append(states[n, :, cols] + spent * total)
        gain = direct[:, cols]

        def body(block, held):
            pair = []
            for part in range(4):
                value = mixed[at_step(block * 4 + part), cols]
                held = [h * r + value for h, r in zip(held, factor)]
                terms = [h * weight[n, :, cols] for n, h in enumerate(held)]
                while len(terms) > 1:
                    terms = [a + b for a, b in zip(terms[::2], terms[1::2])]
                pair.append(terms[0].astype(bf16).astype(f32) + gain * value)
            place = pl.ds(multiple(block * 4 * SEGMENTS, 4 * SEGMENTS), 4 * SEGMENTS)
            kept[place, cols] = jnp.concatenate(pair, axis=0).astype(bf16)
            return held

        lax.fori_loop(0, steps // 4, body, start)

    def give(c, k):
        at = slice(c * strip, (c + 1) * strip)
        here = pl.ds(multiple(peers[k] * rows, rows), rows)
        there = pl.ds(multiple(spot * width + c * strip, strip), strip)
        return go(turned.at[here, at], given.at[:, there], GIVE + 3 * c + k - 1,
                  device(plane, peers[k]))

    def turn(c):
        at = slice(c * strip, (c + 1) * strip)
        turned[:, at] = dot(gather, kept[:, at]).astype(bf16)
        for k in AGAIN:
            give(c, k).start()

    on = p.me > 0

    def product(s, c, block):
        cols = pl.ds(multiple(s * width + c * strip, strip), strip)
        edge = jnp.where(on, query_edge[:, cols].astype(f32), 0.0)
        signal = jnp.concatenate([edge, query[:, cols].astype(f32)], axis=0)
        total = None
        for t in range(count):
            term = taps[0, pl.ds(t, 1), cols] * signal[margin - t:margin - t + rows]
            total = term if total is None else total + term
        out[:, cols] = (total * block.astype(f32)).astype(out.dtype)

    @pl.loop(0, tiles)
    def _(tile):
        mix(tile)
        end_of(tile)
        share(tile)

    for c in range(CUTS):

        @pl.loop(c * (tiles // CUTS), (c + 1) * (tiles // CUTS))
        def _(tile):
            arrive(tile)
            conv(tile)

        turn(c)

    for c in range(CUTS):
        mine_rows = pl.ds(multiple(spot * rows, rows), rows)
        product(spot, c, turned[mine_rows, c * strip:(c + 1) * strip])
    for c in range(CUTS):
        for k in AGAIN:
            give(c, k).wait_recv()
            at = pl.ds(multiple(peers[k] * width + c * strip, strip), strip)
            product(peers[k], c, given[:, at])
    for c in range(CUTS):
        for k in AGAIN:
            give(c, k).wait_send()

    @pl.loop(0, tiles)
    def _(tile):
        for d in AGAIN:
            pl.when(plane + d < GROUP)(ends_copy(tile, d).wait_send)


def talk(kernel, shapes, in_specs, scratch, copies, locals_, ident):
    one = not isinstance(shapes, (list, tuple))
    return pl.pallas_call(
        kernel,
        out_shape=shapes,
        in_specs=in_specs,
        out_specs=ANY if one else [ANY] * len(shapes),
        scratch_shapes=scratch + [
            pltpu.SemaphoreType.DMA((copies,)),
            pltpu.SemaphoreType.DMA((copies,)),
            pltpu.SemaphoreType.DMA((locals_,)),
        ],
        compiler_params=pltpu.CompilerParams(collective_id=ident, has_side_effects=True),
    )


def planes_device(
    tokens, query_in, key_in, proj_in, proj_out, short_taps, residues, mode_rates, skip_gain
):
    rows, channels = tokens.shape
    ranks = proj_in.shape[1]
    modes = residues.shape[0]
    margin_rows = short_taps.shape[1] - 1
    width, all_rows = channels // GROUP, rows * GROUP
    tall = width // 128
    half = jnp.bfloat16
    shape = jax.ShapeDtypeStruct
    plane, spot = where_am_i()
    margin = 16
    share, both = GROUP * ranks, GROUP * GROUP * ranks

    full, band = jnp.float32, rows // 2
    low_all, rows_all, key_all, query_edge = talk(
        fetch_all,
        [shape((margin + all_rows, both), half), shape((GROUP, GROUP, ranks, width), half),
         shape((margin + all_rows, width), half), shape((margin, channels), half)],
        [VMEM] * 5,
        [pltpu.VMEM((both, width), half), pltpu.VMEM((2 * all_rows, width), half),
         pltpu.VMEM((GROUP, GROUP, ranks, width), half), pltpu.VMEM((margin + all_rows, width), half), pltpu.VMEM((margin, channels), half),
         pltpu.VMEM((2, GROUP, 2, band, both), full), pltpu.VMEM((2, GROUP, band, both), full),
         pltpu.VMEM((2, GROUP, band, both), half), pltpu.VMEM((GROUP - 1, 2, band, both), half),
         pltpu.VMEM((band, both), half), pltpu.VMEM((band, both), half),
         pltpu.VMEM((margin + all_rows, both), half)],
        COPIES, 7, 5,
    )(tokens, proj_in.T, proj_out, key_in, query_in)
    spread_rows = all_rows + SEGMENTS * SEGMENTS
    eight = pltpu.VMEM((modes, SEGMENTS, width), full)
    return pl.pallas_call(
        convolve,
        out_shape=shape((rows, channels), half),
        in_specs=[VMEM] * 9, out_specs=VMEM,
        scratch_shapes=[
            pltpu.VMEM((spread_rows, both), half), pltpu.VMEM((spread_rows, width), full),
            pltpu.VMEM((spread_rows, width), full), pltpu.VMEM((all_rows, width), full),
            pltpu.VMEM((all_rows, width), half), pltpu.VMEM((all_rows, width), half),
            pltpu.VMEM((rows, channels), half),
            pltpu.VMEM((2, margin_rows + 1, SEGMENTS, width), full), eight, eight,
            pltpu.VMEM((SEGMENTS, width), full), eight, eight,
            pltpu.VMEM((width // LANES, modes, LANES), full),
            pltpu.VMEM((width // LANES, GROUP - 1, modes, LANES), full),
            pltpu.SemaphoreType.DMA((TAIL_COPIES,)), pltpu.SemaphoreType.DMA((TAIL_COPIES,))],
        compiler_params=pltpu.CompilerParams(collective_id=2, has_side_effects=True),
    )(low_all, rows_all, key_all, query_in, query_edge, short_taps, residues, mode_rates,
      skip_gain[None])


precise = lax.Precision.HIGHEST


def carried_in(value, axis, join, neutral):
    count, mine = (lax.axis_size(axis), lax.axis_index(axis))
    pieces = jax.tree.map(lambda part: lax.all_gather(part, axis), value)
    total = jax.tree.map(
        lambda part, zero: jnp.full_like(part, 0) + jnp.asarray(zero, part.dtype), value, neutral
    )

    def turn(position, total):
        longer = join(total, jax.tree.map(lambda part: part[position], pieces))
        return jax.tree.map(lambda new, old: jnp.where(position < mine, new, old), longer, total)

    return lax.fori_loop(0, count - 1, turn, total)


def passed_along(value, axis, steps):
    count = lax.axis_size(axis)
    leading, last = (max(0, -steps), min(count, count - steps))
    return lax.ppermute(value, axis, [(source, source + steps) for source in range(leading, last)])


def short_filter(previous, current, filter_taps):
    margin_rows = filter_taps.shape[0] - 1
    length = current.shape[0]
    extended = jnp.concatenate([previous, current], axis=0).astype(jnp.float32)
    result = filter_taps[0] * extended[margin_rows : margin_rows + length]
    for offset in range(1, margin_rows + 1):
        result = (
            result
            + filter_taps[offset] * extended[margin_rows - offset : margin_rows - offset + length]
        )
    return result


def carry_states(earlier, later):
    return (earlier[0] * later[1] + later[0], earlier[1] * later[1])


def modal_convolve(mixed, residues, mode_rates):
    tok_rows = mixed.shape[0]
    signal = mixed.astype(jnp.float32)
    steps = jnp.arange(tok_rows, dtype=jnp.int32)
    lower = (steps[:, None] >= steps[None, :]).astype(jnp.float32)
    centred = (steps.astype(jnp.float32) - 0.5 * tok_rows)[:, None]
    local_total = jnp.zeros(signal.shape, jnp.float32)
    end_list = []
    for mode_index in range(residues.shape[0]):
        rate_mode = mode_rates[mode_index]
        weight = residues[mode_index] * jnp.sqrt(rate_mode)
        rising = jnp.exp(rate_mode * centred)
        falling = jnp.exp(-rate_mode * centred)
        running = falling * jnp.dot(lower, rising * signal, precision=precise)
        local_total = local_total + weight * running
        end_list.append(running[tok_rows - 1])
    end_states = jnp.stack(end_list)
    block_decay = jnp.exp(-mode_rates * tok_rows)
    identity = (jnp.zeros(end_states.shape, jnp.float32), jnp.ones(end_states.shape, jnp.float32))
    carried, _ = carried_in((end_states, block_decay), "seq", carry_states, identity)
    after = (steps.astype(jnp.float32) + 1.0)[:, None]
    for mode_index in range(residues.shape[0]):
        rate_mode = mode_rates[mode_index]
        weight = residues[mode_index] * jnp.sqrt(rate_mode)
        local_total = local_total + weight * carried[mode_index] * jnp.exp(-rate_mode * after)
    rounded = lax.optimization_barrier(local_total.astype(jnp.bfloat16))
    return rounded.astype(jnp.float32)


def per_device(
    tokens, query_in, key_in, proj_in, proj_out, short_taps, residues, mode_rates, skip_gain
):
    tok_rows = tokens.shape[0]
    margin_rows = short_taps.shape[1] - 1
    partial_value = jnp.dot(
        tokens,
        lax.all_gather(proj_in, "seq", axis=1, tiled=True),
        preferred_element_type=jnp.float32,
    )
    low_rank = lax.psum(partial_value, "ch").astype(jnp.bfloat16)
    value_full = jnp.dot(
        low_rank,
        lax.all_gather(proj_out, "seq", axis=0, tiled=True),
        preferred_element_type=jnp.float32,
    )
    value_proj = value_full.astype(jnp.bfloat16)
    edges = jnp.stack(
        [
            query_in[tok_rows - margin_rows :],
            key_in[tok_rows - margin_rows :],
            value_proj[tok_rows - margin_rows :],
        ]
    )
    arrived_edges = passed_along(edges, "seq", 1)
    query_previous = arrived_edges[0]
    key_previous = arrived_edges[1]
    value_previous = arrived_edges[2]
    query_short = short_filter(query_previous, query_in, short_taps[0])
    key_short = short_filter(key_previous, key_in, short_taps[1])
    value_short = short_filter(value_previous, value_proj, short_taps[2])
    mixed = (key_short * value_short).astype(jnp.bfloat16)
    convolved_tokens = modal_convolve(mixed, residues, mode_rates)
    return (query_short * (convolved_tokens + skip_gain * mixed.astype(jnp.float32))).astype(
        jnp.bfloat16
    )


def chosen(mesh):
    def run(*args):
        rows, channels = args[0].shape
        ranks = args[3].shape[1]
        square = mesh.shape["seq"] == GROUP * GROUP and mesh.shape["ch"] == 2
        whole = channels % (GROUP * 1024) == 0 and ranks % 32 == 0 and rows % 32 == 0
        fits = (GROUP * ranks) % 128 == 0 and channels == GROUP * 1024
        fits = fits and args[5].shape[1] <= 16
        return (planes_device if square and whole and fits else per_device)(*args)

    return run


def solution(mesh):
    placed = (
        P("seq", "ch"),
        P("seq", "ch"),
        P("seq", "ch"),
        P("ch", "seq"),
        P("seq", "ch"),
        P(None, None, "ch"),
        P(None, "ch"),
        P(None, "ch"),
        P("ch"),
    )
    return jax.shard_map(
        chosen(mesh), mesh=mesh, in_specs=placed, out_specs=P("seq", "ch"), check_vma=False
    )
```

time: 162 us -> 139 us (0.86)
  Pallas kernels: 152 us -> 137 us
  matrix products: 5.22 us -> 0 us
  other arithmetic: 3.02 us -> 0 us
    pallas_call x4 -> x1, Pallas kernels: 43.8 us -> 34.2 us  [planes_device(): pl.pallas_call(convolve, out_shape=shape((rows, channels), half), in_spec...]
    pallas_call x1, Pallas kernels: 108 us -> 102 us  [planes_device(): talk(fetch_all, [shape((margin + all_rows, both), half), shape((GROUP, GR...]
    dot_general x1 -> x0, matrix products: 5.22 us -> none  [planes_device(): jnp.dot(low_all, rows_all.reshape(both, width), preferred_element_type=jn...]
    convert_element_type x2 -> x0, other arithmetic: 3 us -> none  [the longest x1 2.71 us: planes_device(): return (query_short * given.astype(jnp.float32)).astype(half)]
    unnamed x6 -> x1, local copies, waits for them, and re-layouts: 0.01 us -> 2.29 us
where the time goes in v2:
time: 139 us
  Pallas kernels  137 us (99%)
  local copies, waits for them, and re-layouts  2.29 us (2%)
    pallas_call x1, Pallas kernels, planes_device(): talk(fetch_all, [shape((margin + all_rows, both), half), shape((GROUP, GR...  102 us
    pallas_call x1, Pallas kernels, planes_device(): pl.pallas_call(convolve, out_shape=shape((rows, channels), half), in_spec...  34.2 us

profile of v2, /device:TPU:0, one launch (start us, length us, event | category | flops | bytes accessed | tf_op | source)
XLA Modules:
  0.0 139.0 jit_solution(4513520636097290963)
XLA Ops:
  0.0 102.5 %shard_map.91 = (bf16[528,1536]{1,0:T(8,128)(2,1)}, bf16[4,4,96,1024]{3,2,1,0:T(8,128)(2,1)}, bf16[528,1024]{1,0:T(8,128)(2,1)}, bf16[16,4096]{1,0:T(8,128)(2,1)}) custom-call(bf16[128,4096]{1,0:T(8,128)(2,1)} %tok.1, bf16[96,4096]{1,0:T(8,128)(2,1)} %bitcast.2, bf16[96,4096]{1,0:T(8,128)(2,1)} %pout.1, bf16[128,4096]{1,0:T(8,128)(2,1)} %key.1, ...), custom_call_target="tpu_custom_call" | custom-call | tf_op jit(solution)/shard_map/pallas_call | solution.py:696
  102.5 34.2 %shard_map.92 = bf16[128,4096]{1,0:T(8,128)(2,1)} custom-call(bf16[528,1536]{1,0:T(8,128)(2,1)} %get-tuple-element.9.low_all, bf16[4,4,96,1024]{3,2,1,0:T(8,128)(2,1)} %get-tuple-element.10.w2, bf16[528,1024]{1,0:T(8,128)(2,1)} %get-tuple-element.11.key_all, bf16[128,4096]{1,0:T(8,128)(2,1)} %query.3, bf16[16,4096]{1,0:T(8,128)(2,1)} %get-tuple-element.12.query_edge, ...), custom_call_target="tpu_custom_call" | custom-call | tf_op jit(solution)/shard_map/pallas_call | solution.py:711
  136.7 2.3 %copy.11 = bf16[128,4096]{1,0:T(8,128)(2,1)} copy(bf16[128,4096]{1,0:T(8,128)(2,1)} %shard_map.92) | data formatting | bytes 2097152
